TPU v7x, 32 devices: a whole 2x2x4 slice. The times are simulated.
32 devices in a mesh: rep: 2 (over x), section: 2 (over core), wide: 8 (over z, y).
Axes of the slice: x: 2, y: 2, z: 4, core: 2. Of those that a mesh axis runs over, the one named last changes fastest.
Arguments:
- acts: bfloat16 [2, 128, 8192], P('section', 'rep', 'wide'), parts along dimension 1, may hold values from -100 to 100
- norm_gain: bfloat16 [2, 8192], P('section', 'wide'), may hold values from 0.099609375 to 1.8984375
- w_qkv: bfloat16 [2, 8192, 5120], P('section', None, 'wide'), may hold values from -0.0625 to 0.0625
- w_out: bfloat16 [2, 4096, 8192], P('section', None, 'wide'), may hold values from -0.5 to 0.5
- key_cache: bfloat16 [2, 128, 384, 512], P('section', ('rep', 'wide')), parts along dimension 1, may hold values from -400 to 400
- value_cache: bfloat16 [2, 128, 384, 512], P('section', ('rep', 'wide')), parts along dimension 1, may hold values from -6 to 6
- cache_lengths: int32 [2, 128], P('section', ('rep', 'wide')), parts along dimension 1, may hold values from 2 to 384, as said below
- slot_of: int32 [2, 128], P('section', 'rep'), parts along dimension 1, may hold values from 0 to 63, each once within a row
Outputs:
- handed: bfloat16 [2, 128, 8192], P('section', 'rep', 'wide'), parts along dimension 1
There are 2 independent parts, one for each index of `rep`. A program takes and returns all parts, laid end to end along the dimension named above; an argument that names none is the same for every part. Nothing has to cross between parts.
Inputs may be any that keep to these rules, and one draw needn't show every extreme that they name: `cache_lengths`: slot j of a section belongs to owner j // 8; in every section some slot holds exactly 384. `slot_of`: each section's row names every slot once.
All inputs are finite; a program needn't handle non-finite values.
Results may differ from a plain program's by a relative error of at most 0.005.
Values may be sent and summed in bfloat16 or wider, within the bound.
A program may use at most 64 MiB of HBM per device.

v0:
```python
import math

import jax
import jax.numpy as jnp
from jax import lax
from jax.sharding import PartitionSpec as P

D = 8192
HEADS = 32
KV_HEADS = 4
HDIM = 128


epsilon = 1e-05
rope_base = 500000.0
masked_score = -1e30


def passed_along(value, axis, steps):
    count = lax.axis_size(axis)
    pairs = [(source, (source + steps) % count) for source in range(count)]
    return lax.ppermute(value, axis, pairs)


def rotate(values, position):
    half_dim = HDIM // 2
    exponent = jnp.arange(half_dim, dtype=jnp.float32) * (2.0 / HDIM)
    frequency = jnp.exp(-math.log(rope_base) * exponent)
    angle = position[..., None] * frequency
    cosine = jnp.cos(angle)
    sine = jnp.sin(angle)
    first_half = values[..., :half_dim]
    second_half = values[..., half_dim:]
    return jnp.concatenate(
        [first_half * cosine - second_half * sine, second_half * cosine + first_half * sine],
        axis=-1,
    )


def attend(joined_rows, key_rows, value_rows, lengths_here):
    row_count = joined_rows.shape[0]
    groups = HEADS // KV_HEADS
    query_width = HEADS * HDIM
    kv_width = KV_HEADS * HDIM
    queries = joined_rows[:, :query_width].reshape(row_count, KV_HEADS, groups, HDIM)
    new_keys = joined_rows[:, query_width : query_width + kv_width].reshape(
        row_count, KV_HEADS, HDIM
    )
    new_values = joined_rows[:, query_width + kv_width :].reshape(row_count, KV_HEADS, HDIM)
    position = lengths_here.astype(jnp.float32)
    queries = rotate(queries.astype(jnp.float32), position[:, None, None]).astype(jnp.bfloat16)
    new_keys = rotate(new_keys.astype(jnp.float32), position[:, None]).astype(jnp.bfloat16)
    score_scale = 1.0 / math.sqrt(HDIM)
    cache_span = key_rows.shape[1]
    cached_keys = key_rows.reshape(row_count, cache_span, KV_HEADS, HDIM)
    cached_values = value_rows.reshape(row_count, cache_span, KV_HEADS, HDIM)
    own_score = (
        jnp.einsum("ngqd,ngd->ngq", queries, new_keys, preferred_element_type=jnp.float32)
        * score_scale
    )
    scores = (
        jnp.einsum("ngqd,nlgd->ngql", queries, cached_keys, preferred_element_type=jnp.float32)
        * score_scale
    )
    live_mask = (jnp.arange(cache_span, dtype=jnp.int32)[None, :] < lengths_here[:, None])[
        :, None, None, :
    ]
    masked = jnp.where(live_mask, scores, masked_score)
    peak = jnp.maximum(jnp.max(masked, axis=-1), own_score)
    weights = jnp.where(live_mask, jnp.exp(masked - peak[..., None]), 0.0)
    sums = jnp.sum(weights, axis=-1)
    weighted = jnp.einsum(
        "ngql,nlgd->ngqd",
        weights.astype(jnp.bfloat16),
        cached_values,
        preferred_element_type=jnp.float32,
    )
    own_weight = jnp.exp(own_score - peak)
    denominator = sums + own_weight
    own_rounded = own_weight.astype(jnp.bfloat16).astype(jnp.float32)
    weighted = weighted + own_rounded[..., None] * new_values.astype(jnp.float32)[:, :, None, :]
    return (weighted / denominator[..., None]).reshape(row_count, query_width).astype(jnp.bfloat16)


def shards(acts, norm_gain, w_qkv, w_out, key_cache, value_cache, cache_lengths, slot_of):
    tokens = acts[0].astype(jnp.float32)
    squares = lax.psum(jnp.sum(tokens * tokens, axis=1), "wide")
    normed = (
        tokens * lax.rsqrt(squares / D + epsilon)[:, None] * norm_gain[0].astype(jnp.float32)
    ).astype(jnp.bfloat16)
    slot_table = slot_of[0]
    request_total = slot_table.shape[0]
    request_at_slot = (
        jnp.zeros((request_total,), jnp.int32)
        .at[slot_table]
        .set(jnp.arange(request_total, dtype=jnp.int32))
    )
    projection = w_qkv[0]
    whole = lax.all_gather(normed, "wide", axis=1, tiled=True)
    columns = jnp.dot(whole, projection, preferred_element_type=jnp.float32).astype(jnp.bfloat16)
    joined_rows = lax.all_to_all(
        columns[request_at_slot], "wide", split_axis=0, concat_axis=1, tiled=True
    )
    attended = attend(joined_rows, key_cache[0], value_cache[0], cache_lengths[0])
    out_weight = w_out[0]
    projected = jnp.dot(
        lax.all_gather(attended, "wide", axis=0, tiled=True),
        out_weight,
        preferred_element_type=jnp.float32,
    )
    updated = (tokens + projected[slot_table]).astype(jnp.bfloat16)
    return passed_along(updated[None], "section", 1)


def solution(mesh):
    placed = (
        P("section", "rep", "wide"),
        P("section", "wide"),
        P("section", None, "wide"),
        P("section", None, "wide"),
        P("section", ("rep", "wide"), None, None),
        P("section", ("rep", "wide"), None, None),
        P("section", ("rep", "wide")),
        P("section", "rep"),
    )
    return jax.shard_map(
        shards, mesh=mesh, in_specs=placed, out_specs=P("section", "rep", "wide"), check_vma=False
    )
```

profile of v0, /device:TPU:0, one launch (start us, length us, event | category | flops | bytes accessed | tf_op | source)
XLA Modules:
  0.0 140.7 jit_solution(9356426057554697303)
XLA Ops:
  6.5 0.0 all-gather.2.cloned.1.call-start
  6.5 0.7 mul.188
  7.2 1.0 fusion.33
  8.3 23.2 %psum.7 = f32[64]{0:T(128)S(1)} all-reduce(f32[64]{0:T(128)S(1)} %fusion.33), channel_id=1, replica_groups=mesh['rep'=2,'section'=2,'wide'=8] {'wide'}, use_global_device_ids=true, to_apply=%region_1.0 | all-reduce | flops 64 | bytes 512 | tf_op jit(solution)/shard_map/psum | solution.py:87
  31.4 1.7 %fusion.35 = bf16[64,1024]{1,0:T(8,128)(2,1)} fusion(bf16[1,64,1024]{2,1,0:T(8,128)(2,1)} %param.8, f32[1024]{0:T(1024)S(1)} %bitcast.71, f32[64]{0:T(128)S(1)} %add_rsqrt_fusion), kind=kLoop, calls=%fused_computation.27 | loop fusion | flops 262144 | bytes 266496 | tf_op jit(solution)/shard_map/convert_element_type | solution.py:90
  33.1 0.0 all-gather.2.cloned.1.call-update
  33.1 0.7 fusion.46
  33.8 0.8 scatter_custom_fusion
  34.6 0.7 bitcast_convert_fusion
  35.3 0.1 multiply_cosine_fusion
  35.4 0.0 copy-start.2
  35.4 35.4 %all-gather.2.cloned.1.call-done = bf16[64,8192]{1,0:T(8,128)(2,1)} async-done(((bf16[64,1024]{1,0:T(8,128)(2,1)}), bf16[64,8192]{1,0:T(8,128)(2,1)}) %all-gather.2.cloned.1.call-update) | async-done | bytes 1048592 | tf_op jit(solution)/shard_map/all_gather | solution.py:99
  70.8 6.1 %fusion.20 = bf16[64,640]{1,0:T(8,128)(2,1)S(1)} fusion(bf16[64,8192]{1,0:T(8,128)(2,1)} %all-gather.2.cloned.1.call-done, bf16[1,8192,640]{2,1,0:T(8,128)(2,1)} %param.10), kind=kOutput, calls=%fused_computation.15 | convolution fusion | flops 671129600 | bytes 11616256 | tf_op jit(solution)/shard_map/dot_general | solution.py:100
  76.9 1.3 gather_fusion
  78.3 3.4 %all-to-all-start = ((bf16[8,8,640]{2,1,0:T(8,128)(2,1)}), bf16[8,8,640]{2,1,0:T(8,128)(2,1)S(1)}, u32[]{:S(2)}, u32[]{:S(2)}) async-start(bf16[8,8,640]{2,1,0:T(8,128)(2,1)} %bitcast.6), calls=%async_computation | async-start | bytes 163840 | tf_op jit(solution)/shard_map/all_to_all | solution.py:101
  81.6 0.1 iota_compare_fusion
  81.7 3.8 %reshape_squeeze.6 = bf16[8,384,4,128]{3,2,1,0:T(4,128)(2,1)S(1)} reshape(bf16[1,8,384,512]{3,2,1,0:T(8,128)(2,1)} %param.12) | data formatting | bytes 6291456 | tf_op jit(solution)/shard_map/reshape;squeeze | solution.py:55
  85.5 5.5 %reshape_squeeze.7 = bf16[8,384,4,128]{3,2,1,0:T(4,128)(2,1)} reshape(bf16[1,8,384,512]{3,2,1,0:T(8,128)(2,1)} %param.13) | data formatting | bytes 6291456 | tf_op jit(solution)/shard_map/reshape;squeeze | solution.py:56
  91.0 0.0 all-to-all-done
  91.1 0.1 subtract_convert_fusion.1
  91.2 0.1 subtract_convert_fusion
  91.3 0.1 maximum_bitcast_fusion
  91.3 0.2 fusion.41
  91.6 1.3 fusion.52
  92.9 0.2 fusion.31
  93.2 0.7 fusion.26
  94.0 32.1 %all_gather.7 = bf16[64,4096]{1,0:T(8,128)(2,1)S(1)} all-gather(bf16[8,4096]{1,0:T(8,128)(2,1)S(1)} %bitcast.68), channel_id=1, replica_groups=mesh['rep'=2,'section'=2,'wide'=8] {'wide'}, dimensions={0}, use_global_device_ids=true | all-gather | bytes 589824 | tf_op jit(solution)/shard_map/all_gather | solution.py:107
  126.1 5.0 %fusion.2 = f32[64,1024]{1,0:T(8,128)S(1)} fusion(bf16[64,4096]{1,0:T(8,128)(2,1)S(1)} %all_gather.7, bf16[1,4096,1024]{2,1,0:T(8,128)(2,1)} %param.11), kind=kOutput, calls=%fused_computation.5 | convolution fusion | flops 536870912 | bytes 9175040 | tf_op jit(solution)/shard_map/dot_general | solution.py:106
  131.1 0.7 gather_fusion.1
  131.8 0.1 collective-permute-start
  131.9 1.3 collective-permute-done
  133.2 0.7 copy.41
  (19 shorter events, 0.2 us)
Async XLA Ops:
  6.5 64.2 %all-gather.2.cloned.1.call-start = ((), (), s32[]{:S(2)}) async-start(), calls=%async_computation.1 | async-start | bytes 1179648 | tf_op jit(solution)/shard_map/all_gather | solution.py:99
  35.4 46.3 %copy-start.2 = (s32[1,8]{1,0:T(1,128)S(1)}, s32[1,8]{1,0:T(1,128)}, u32[]{:S(2)}) copy-start(s32[1,8]{1,0:T(1,128)} %param.14) | copy-start | bytes 100
  78.3 12.7 %all-to-all-start = ((bf16[8,8,640]{2,1,0:T(8,128)(2,1)}), bf16[8,8,640]{2,1,0:T(8,128)(2,1)S(1)}, u32[]{:S(2)}, u32[]{:S(2)}) async-start(bf16[8,8,640]{2,1,0:T(8,128)(2,1)} %bitcast.6), calls=%async_computation | async-start | bytes 163840 | tf_op jit(solution)/shard_map/all_to_all | solution.py:101
  91.0 2.2 %copy-start = (bf16[8,384,4,128]{3,2,1,0:T(4,128)(2,1)S(1)}, bf16[8,384,4,128]{3,2,1,0:T(4,128)(2,1)}, u32[]{:S(2)}) copy-start(bf16[8,384,4,128]{3,2,1,0:T(4,128)(2,1)} %reshape_squeeze.7) | copy-start | bytes 9437188
  126.1 5.7 %copy-start.1 = (bf16[1,64,1024]{2,1,0:T(8,128)(2,1)S(1)}, bf16[1,64,1024]{2,1,0:T(8,128)(2,1)}, u32[]{:S(2)}) copy-start(bf16[1,64,1024]{2,1,0:T(8,128)(2,1)} %param.8) | copy-start | bytes 393220
  131.8 1.4 %collective-permute-start = (bf16[1,64,1024]{2,1,0:T(8,128)(2,1)S(1)}, bf16[1,64,1024]{2,1,0:T(8,128)(2,1)S(1)}, u32[]{:S(2)}, u32[]{:S(2)}) collective-permute-start(bf16[1,64,1024]{2,1,0:T(8,128)(2,1)S(1)} %fusion.36), channel_id=1, source_target_pairs={{0,8},{8,0},{1,9},{9,1},{2,10},{10,2},{3,11},{11,3},{4,12},{12,4},... | collective-permute-start | bytes 393224 | tf_op jit(solution)/shard_map/ppermute | solution.py:22
Sparse Core Ops, SparseCore 0:
  33.2 37.5 all-gather.1
where the time goes:
time: 141 us
  blocking collectives  55.2 us (39%)
  waiting for transfers between devices  36.8 us (26%)
  between operations  13.6 us (10%)
  matrix products  13.4 us (10%)
  local copies, waits for them, and re-layouts  12.8 us (9%)
  other arithmetic  5.5 us (4%)
  starting transfers between devices  3.43 us (2%)
    all_gather x1, waiting for transfers between devices, shards(): whole = lax.all_gather(normed, 'wide', axis=1, tiled=True)  35.4 us
    all_gather x1, blocking collectives, shards(): lax.all_gather(attended, 'wide', axis=0, tiled=True)  32.1 us
    psum x1, blocking collectives, shards(): squares = lax.psum(jnp.sum(tokens * tokens, axis=1), 'wide')  23.2 us
    dot_general x1, matrix products, shards(): jnp.dot(whole, projection, preferred_element_type=jnp.float32)  6.12 us
    another operation x1, local copies, waits for them, and re-layouts, attend(): cached_values = value_rows.reshape(row_count, cache_span, KV_HEADS, HDIM)  5.52 us
    dot_general x1, matrix products, shards(): jnp.dot(lax.all_gather(attended, 'wide', axis=0, tiled=True), out_weight,...  5 us
    another operation x1, local copies, waits for them, and re-layouts, attend(): cached_keys = key_rows.reshape(row_count, cache_span, KV_HEADS, HDIM)  3.75 us
    all_to_all x1, starting transfers between devices, shards(): lax.all_to_all(columns[request_at_slot], 'wide', split_axis=0, concat_axi...  3.36 us
  transfers between devices with their start and end apart: 3, of which 2 were waited for; matrix products, arithmetic and copies ran while one was open for 8% of the time, Pallas kernels for 0%

commit v1 on v0

--- a/solution.py
+++ b/solution.py
@@ -1,8 +1,11 @@
+import functools
 import math
 
 import jax
 import jax.numpy as jnp
 from jax import lax
+from jax.experimental import pallas as pl
+from jax.experimental.pallas import tpu as pltpu
 from jax.sharding import PartitionSpec as P
 
 D = 8192
@@ -10,10 +13,338 @@
 KV_HEADS = 4
 HDIM = 128
 
-
 epsilon = 1e-05
 rope_base = 500000.0
 masked_score = -1e30
+
+MESH = pl.DeviceIdType.MESH
+
+
+def tick(
+    n, Y, C, sections,
+    acts_ref, gain_ref, slot_ref, len_ref, wq_hbm, wo_hbm, k_hbm, v_hbm, out_hbm,
+    wq, wo, kc, vc, xa, acc, js, jr, sqs, sqr, qs, at, ga, res,
+    wq_sem, wo_sem, k_sem, v_sem,
+    x_sz, x_sy, x_rv, j_sn, j_rv, q_sn, q_rv, a_sz, a_sy, a_rv, o_sn, o_rv,
+):
+    me = lax.axis_index("wide")
+    sec = lax.axis_index("section")
+    Z = n // Y
+    z, y = me // Y, lax.rem(me, Y)
+    other = z * Y + (1 - y)
+    rows, width = acts_ref.shape[1], acts_ref.shape[2]
+    CK = width // C
+    G = KV_HEADS
+    heads = HEADS // G
+    own = rows // n
+    cols = wq.shape[1]
+    slabs = cols // HDIM
+    out_chunks = res.shape[0]
+    OC = res.shape[2]
+
+    barrier = pltpu.get_barrier_semaphore()
+    for step in range(1, n):
+        pl.semaphore_signal(
+            barrier, inc=1, device_id={"wide": lax.rem(me + step, n)}, device_id_type=MESH
+        )
+    pl.semaphore_signal(
+        barrier, inc=1, device_id={"section": lax.rem(sec + 1, sections)}, device_id_type=MESH
+    )
+
+    def wq_copy(b):
+        at_rows = pl.ds(pl.multiple_of(b * width, width), width)
+        return pltpu.make_async_copy(wq_hbm.at[0, at_rows, :], wq.at[at_rows, :], wq_sem.at[b])
+
+    for step in range(n):
+        wq_copy(lax.rem(me + step, n)).start()
+    k_copy = pltpu.make_async_copy(k_hbm.at[0], kc, k_sem)
+    v_copy = pltpu.make_async_copy(v_hbm.at[0], vc, v_sem)
+    wo_copy = pltpu.make_async_copy(wo_hbm.at[0], wo, wo_sem)
+    k_copy.start()
+    v_copy.start()
+    wo_copy.start()
+
+    tokens = acts_ref[0].astype(jnp.float32)
+    gained = (tokens * gain_ref[...].astype(jnp.float32)).astype(jnp.bfloat16)
+    for c in range(C):
+        xa[me, c] = gained[:, c * CK : (c + 1) * CK]
+    squares = jnp.sum(tokens * tokens, axis=1, keepdims=True)
+    sub = lax.broadcasted_iota(jnp.int32, (rows, rows), 0)
+    lane = lax.broadcasted_iota(jnp.int32, (rows, rows), 1)
+    square_row = jnp.sum(jnp.where(sub == lane, squares, 0.0), axis=0, keepdims=True)
+    to_slot_mask = sub == slot_ref[...]
+    square_slot = jnp.sum(jnp.where(to_slot_mask, square_row, 0.0), axis=1, keepdims=True)
+    square_wide = jnp.broadcast_to(square_slot, (rows, HDIM))
+    for o in range(n):
+        sqs[o] = square_wide[o * own : (o + 1) * own]
+    to_slot_f = jnp.where(to_slot_mask, 1.0, 0.0)
+    to_slot = to_slot_f.astype(jnp.bfloat16)
+    to_request = to_slot_f.T.astype(jnp.bfloat16)
+
+    pl.semaphore_wait(barrier, n)
+
+    def remote(src, dst, send, recv, target):
+        return pltpu.make_async_remote_copy(
+            src_ref=src, dst_ref=dst, send_sem=send, recv_sem=recv,
+            device_id={"wide": target}, device_id_type=MESH,
+        )
+
+    def x_z(dz, c):
+        return remote(
+            xa.at[me, c], xa.at[me, c], x_sz.at[dz, c], x_rv.at[me, c],
+            lax.rem(z + dz, Z) * Y + y,
+        )
+
+    def x_y(zb, c):
+        b = zb * Y + y
+        return remote(xa.at[b, c], xa.at[b, c], x_sy.at[zb, c], x_rv.at[b, c], other)
+
+    def x_wait(b, c):
+        remote(xa.at[b, c], xa.at[b, c], x_sy.at[0, c], x_rv.at[b, c], other).wait_recv()
+
+    for c in range(C):
+        x_y(z, c).start()
+        for dz in range(1, Z):
+            x_z(dz, c).start()
+
+    def q_copy(step):
+        o = lax.rem(me + step, n)
+        return remote(sqs.at[o], sqr.at[me], q_sn.at[step], q_rv.at[me], o)
+
+    for step in range(1, n):
+        q_copy(step).start()
+    sqr[me] = sqs[me]
+
+    def piece(b, c):
+        at_rows = pl.ds(pl.multiple_of(b * width + c * CK, CK), CK)
+        return jnp.dot(xa[b, c], wq[at_rows, :], preferred_element_type=jnp.float32)
+
+    for step in range(n):
+        wq_copy(lax.rem(me + step, n)).wait()
+
+    total = piece(me, 0)
+    for c in range(1, C):
+        total += piece(me, c)
+    acc[...] = total
+
+    def other_line(c):
+        for dz in range(Z):
+            x_wait(lax.rem(z + dz, Z) * Y + (1 - y), c)
+        part = acc[...]
+        for dz in range(Z):
+            part += piece(lax.rem(z + dz, Z) * Y + (1 - y), c)
+        acc[...] = part
+
+    def gather_step(c, carry):
+        for dz in range(1, Z):
+            zb = lax.rem(z + dz, Z)
+            x_wait(zb * Y + y, c)
+            x_y(zb, c).start()
+        part = acc[...]
+        for dz in range(1, Z):
+            part += piece(lax.rem(z + dz, Z) * Y + y, c)
+        acc[...] = part
+
+        @pl.when(c > 0)
+        def _():
+            other_line(c - 1)
+
+        return carry
+
+    lax.fori_loop(0, C, gather_step, 0)
+    other_line(C - 1)
+
+    by_slot = jnp.dot(to_slot, acc[...].astype(jnp.bfloat16), preferred_element_type=jnp.float32)
+    for o in range(n):
+        js[o] = by_slot[o * own : (o + 1) * own].astype(jnp.bfloat16)
+
+    def j_copy(step):
+        o = lax.rem(me + step, n)
+        return remote(js.at[o], jr.at[me], j_sn.at[step], j_rv.at[me], o)
+
+    for step in range(1, n):
+        j_copy(step).start()
+    jr[me] = js[me]
+
+    row_of = lax.broadcasted_iota(jnp.int32, (own, HDIM), 0)
+    lane_of = lax.broadcasted_iota(jnp.int32, (own, HDIM), 1)
+    position = jnp.zeros((own, HDIM), jnp.int32)
+    for r in range(own):
+        position = jnp.where(row_of == r, len_ref[0, r], position)
+    half = lax.rem(lane_of, HDIM // 2).astype(jnp.float32) * (2.0 / HDIM)
+    angle = position.astype(jnp.float32) * jnp.exp(-math.log(rope_base) * half)
+    cosine = jnp.cos(angle)
+    sine = jnp.where(lane_of < HDIM // 2, -jnp.sin(angle), jnp.sin(angle))
+    k_copy.wait()
+    v_copy.wait()
+    wo_copy.wait()
+
+    for step in range(1, n):
+        b = lax.rem(me + step, n)
+        remote(sqs.at[b], sqr.at[b], q_sn.at[step], q_rv.at[b], b).wait_recv()
+    square_sum = sqr[0]
+    for b in range(1, n):
+        square_sum += sqr[b]
+    scale = lax.rsqrt(square_sum / D + epsilon)
+    for step in range(1, n):
+        b = lax.rem(me + step, n)
+        remote(js.at[b], jr.at[b], j_sn.at[step], j_rv.at[b], b).wait_recv()
+    for b in range(n):
+        for k in range(slabs):
+            feature = b * slabs + k
+            slab = jr[b, :, k * HDIM : (k + 1) * HDIM].astype(jnp.float32) * scale
+            if feature < HEADS + G:
+                turned = slab * cosine + pltpu.roll(slab, HDIM // 2, 1) * sine
+                slab = turned.astype(jnp.bfloat16).astype(jnp.float32)
+            else:
+                slab = slab.astype(jnp.bfloat16).astype(jnp.float32)
+            qs[:, feature, :] = slab
+
+    def a_z(g, dz):
+        return remote(
+            ga.at[g, me], ga.at[g, me], a_sz.at[g, dz], a_rv.at[g, me],
+            lax.rem(z + dz, Z) * Y + y,
+        )
+
+    def a_y(g, zb):
+        b = zb * Y + y
+        return remote(ga.at[g, b], ga.at[g, b], a_sy.at[g, zb], a_rv.at[g, b], other)
+
+    def a_wait(g, b):
+        remote(ga.at[g, b], ga.at[g, b], a_sy.at[g, 0], a_rv.at[g, b], other).wait_recv()
+
+    def relay(g):
+        for dz in range(1, Z):
+            zb = lax.rem(z + dz, Z)
+            a_wait(g, zb * Y + y)
+            a_y(g, zb).start()
+
+    span = kc.shape[1]
+    score_scale = 1.0 / math.sqrt(HDIM)
+    place = lax.broadcasted_iota(jnp.int32, (heads, span), 1)
+    for g in range(G):
+        lanes = slice(g * HDIM, (g + 1) * HDIM)
+        for r in range(own):
+            query = qs[r, g * heads : (g + 1) * heads, :]
+            new_key = qs[r, HEADS + g : HEADS + g + 1, :]
+            new_value = qs[r, HEADS + G + g : HEADS + G + g + 1, :]
+            own_score = jnp.sum(query * new_key, axis=1, keepdims=True) * score_scale
+            scores = (
+                lax.dot_general(
+                    query.astype(jnp.bfloat16), kc[r, :, lanes], (((1,), (1,)), ((), ())),
+                    preferred_element_type=jnp.float32,
+                )
+                * score_scale
+            )
+            live = place < len_ref[0, r]
+            masked = jnp.where(live, scores, masked_score)
+            peak = jnp.maximum(jnp.max(masked, axis=1, keepdims=True), own_score)
+            weights = jnp.where(live, jnp.exp(masked - peak), 0.0)
+            own_weight = jnp.exp(own_score - peak)
+            denominator = jnp.sum(weights, axis=1, keepdims=True) + own_weight
+            weighted = jnp.dot(
+                weights.astype(jnp.bfloat16), vc[r, :, lanes], preferred_element_type=jnp.float32
+            )
+            weighted += own_weight.astype(jnp.bfloat16).astype(jnp.float32) * new_value
+            at[g, r] = weighted / denominator
+        for h in range(heads):
+            ga[g, me, :, h * HDIM : (h + 1) * HDIM] = at[g, :, h, :].astype(jnp.bfloat16)
+        a_y(g, z).start()
+        for dz in range(1, Z):
+            a_z(g, dz).start()
+        if g >= 2:
+            relay(g - 2)
+    for g in range(max(G - 2, 0), G):
+        relay(g)
+
+    def o_copy(c):
+        return pltpu.make_async_remote_copy(
+            src_ref=res.at[c],
+            dst_ref=out_hbm.at[0, :, pl.ds(c * OC, OC)],
+            send_sem=o_sn.at[c],
+            recv_sem=o_rv.at[c],
+            device_id={"section": lax.rem(sec + 1, sections)},
+            device_id_type=MESH,
+        )
+
+    depth = heads * HDIM
+    mixed = []
+    for g in range(G):
+        for dz in range(Z):
+            a_wait(g, lax.rem(z + dz, Z) * Y + (1 - y))
+        block = ga[g].astype(jnp.float32).reshape(rows, depth).astype(jnp.bfloat16)
+        mixed.append(
+            jnp.dot(to_request, block, preferred_element_type=jnp.float32).astype(jnp.bfloat16)
+        )
+        if g == G - 1:
+            whole = jnp.concatenate(mixed, axis=1)
+            for c in range(out_chunks):
+                at_cols = slice(c * OC, (c + 1) * OC)
+                part = acts_ref[0, :, at_cols].astype(jnp.float32)
+                part += jnp.dot(whole, wo[:, at_cols], preferred_element_type=jnp.float32)
+                res[c] = part.astype(jnp.bfloat16)
+                o_copy(c).start()
+
+    for c in range(C):
+        for dz in range(1, Z):
+            x_z(dz, c).wait_send()
+        for zb in range(Z):
+            x_y(zb, c).wait_send()
+    for step in range(1, n):
+        q_copy(step).wait_send()
+        j_copy(step).wait_send()
+    for g in range(G):
+        for dz in range(1, Z):
+            a_z(g, dz).wait_send()
+        for zb in range(Z):
+            a_y(g, zb).wait_send()
+    for c in range(out_chunks):
+        o_copy(c).wait()
+
+
+def fused(n, sections, acts, norm_gain, w_qkv, w_out, key_cache, value_cache, cache_lengths, slot_of):
+    Y, C, out_chunks = 2, 4, 4
+    rows, width = acts.shape[1:]
+    own, span, kv_width = key_cache.shape[1:]
+    cols = w_qkv.shape[2]
+    G = KV_HEADS
+    heads = HEADS // G
+    Z = n // Y
+    vmem = pl.BlockSpec(memory_space=pltpu.VMEM)
+    smem = pl.BlockSpec(memory_space=pltpu.SMEM)
+    anywhere = pl.BlockSpec(memory_space=pl.ANY)
+    bf16, f32 = jnp.bfloat16, jnp.float32
+    dma = pltpu.SemaphoreType.DMA
+    return pl.pallas_call(
+        functools.partial(tick, n, Y, C, sections),
+        out_shape=jax.ShapeDtypeStruct(acts.shape, bf16),
+        in_specs=[vmem, vmem, vmem, smem, anywhere, anywhere, anywhere, anywhere],
+        out_specs=anywhere,
+        scratch_shapes=[
+            pltpu.VMEM(w_qkv.shape[1:], bf16),
+            pltpu.VMEM(w_out.shape[1:], bf16),
+            pltpu.VMEM(key_cache.shape[1:], bf16),
+            pltpu.VMEM(value_cache.shape[1:], bf16),
+            pltpu.VMEM((n, C, rows, width // C), bf16),
+            pltpu.VMEM((rows, cols), f32),
+            pltpu.VMEM((n, own, cols), bf16),
+            pltpu.VMEM((n, own, cols), bf16),
+            pltpu.VMEM((n, own, HDIM), f32),
+            pltpu.VMEM((n, own, HDIM), f32),
+            pltpu.VMEM((own, HEADS + 2 * G, HDIM), f32),
+            pltpu.VMEM((G, own, heads, HDIM), f32),
+            pltpu.VMEM((G, n, own, heads * HDIM), bf16),
+            pltpu.VMEM((out_chunks, rows, width // out_chunks), bf16),
+            dma((n,)), dma, dma, dma,
+            dma((Z, C)), dma((Z, C)), dma((n, C)),
+            dma((n,)), dma((n,)), dma((n,)), dma((n,)),
+            dma((G, Z)), dma((G, Z)), dma((G, n)),
+            dma((out_chunks,)), dma((out_chunks,)),
+        ],
+        compiler_params=pltpu.CompilerParams(
+            collective_id=0, has_side_effects=True, vmem_limit_bytes=60 * 1024 * 1024
+        ),
+    )(acts, norm_gain, slot_of, cache_lengths, w_qkv, w_out, key_cache, value_cache)
 
 
 def passed_along(value, axis, steps):
@@ -123,6 +454,15 @@
         P("section", ("rep", "wide")),
         P("section", "rep"),
     )
+    n, sections = mesh.shape["wide"], mesh.shape["section"]
+
+    def body(*blocks):
+        acts, w_qkv, w_out = blocks[0], blocks[2], blocks[3]
+        aligned = acts.shape[2] % 1024 == 0 and w_qkv.shape[2] % HDIM == 0
+        if n % 2 == 0 and aligned and blocks[4].shape[1] * n == acts.shape[1]:
+            return fused(n, sections, *blocks)
+        return shards(*blocks)
+
     return jax.shard_map(
-        shards, mesh=mesh, in_specs=placed, out_specs=P("section", "rep", "wide"), check_vma=False
-    )
+        body, mesh=mesh, in_specs=placed, out_specs=P("section", "rep", "wide"), check_vma=False
+    )

time: 141 us -> 52.5 us (0.37)
  blocking collectives: 55.2 us -> 0 us
  Pallas kernels: 0 us -> 50.8 us
  waiting for transfers between devices: 36.8 us -> 0 us
  between operations: 13.6 us -> 0.01 us
  matrix products: 13.4 us -> 0 us
  local copies, waits for them, and re-layouts: 12.8 us -> 1.57 us
  other arithmetic: 5.5 us -> 0 us
  starting transfers between devices: 3.43 us -> 0 us
    pallas_call x0 -> x1, Pallas kernels: none -> 50.8 us  [fused(): pl.pallas_call(functools.partial(tick, n, Y, C, sections), out_shape=jax....]
    all_gather x1 -> x0, waiting for transfers between devices: 35.4 us -> none  [shards(): whole = lax.all_gather(normed, 'wide', axis=1, tiled=True)]
    all_gather x1 -> x0, blocking collectives: 32.1 us -> none  [shards(): lax.all_gather(attended, 'wide', axis=0, tiled=True)]
    psum x1 -> x0, blocking collectives: 23.2 us -> none  [shards(): squares = lax.psum(jnp.sum(tokens * tokens, axis=1), 'wide')]
    dot_general x5 -> x0, matrix products: 13.4 us -> none  [the longest x1 6.12 us: shards(): jnp.dot(whole, projection, preferred_element_type=jnp.float32)]
    another operation x2 -> x0, local copies, waits for them, and re-layouts: 9.27 us -> none  [the longest x1 5.52 us: attend(): cached_values = value_rows.reshape(row_count, cache_span, KV_HEADS, HDIM)]
    all_to_all x1 -> x0, starting transfers between devices: 3.36 us -> none  [shards(): lax.all_to_all(columns[request_at_slot], 'wide', split_axis=0, concat_axi...]
    convert_element_type x5 -> x0, other arithmetic: 2.37 us -> none  [the longest x1 1.66 us: shards(): normed = (tokens * lax.rsqrt(squares / D + epsilon)[:, None] * norm_gain[...]
  transfers between devices with their start and end apart: 3 -> 0, of which waited for: 2 -> 0; matrix products, arithmetic and copies ran while one was open for 8% -> 0% of each run, Pallas kernels for 0% -> 0%
where the time goes in v1:
time: 52.5 us; the launch traced here: 52.4 us
  Pallas kernels  50.8 us (97%)
  local copies, waits for them, and re-layouts  1.57 us (3%)
    pallas_call x1, Pallas kernels, fused(): pl.pallas_call(functools.partial(tick, n, Y, C, sections), out_shape=jax....  50.8 us
    unnamed x1, local copies, waits for them, and re-layouts  1.57 us

profile of v1, /device:TPU:0, one launch (start us, length us, event | category | flops | bytes accessed | tf_op | source)
XLA Modules:
  0.0 52.4 jit_solution(15146224335047293460)
XLA Ops:
  0.0 50.8 %shard_map.82 = bf16[1,64,1024]{2,1,0:T(8,128)(2,1)} custom-call(bf16[1,64,1024]{2,1,0:T(8,128)(2,1)} %acts_ref.1, bf16[1,1024]{1,0:T(2,128)(2,1)} %gain_ref.1, s32[1,64]{1,0:T(1,128)} %slot_ref.1, s32[1,8]{1,0:T(1,128)} %len_ref.1, bf16[1,8192,640]{2,1,0:T(8,128)(2,1)} %wq_hbm.1, bf16[1,4096,1024]{2,1,0:T(8,128)(2,1)} %wo_hbm.1, ...), custom_call_target="tpu_custom_call" | custom-call | tf_op jit(solution)/shard_map/pallas_call | solution.py:318
  50.8 1.6 %copy.10 = bf16[1,64,1024]{2,1,0:T(8,128)(2,1)} copy(bf16[1,64,1024]{2,1,0:T(8,128)(2,1)} %shard_map.82) | data formatting | bytes 262144

commit v2 on v1

--- a/solution.py
+++ b/solution.py
@@ -23,7 +23,7 @@
 def tick(
     n, Y, C, sections,
     acts_ref, gain_ref, slot_ref, len_ref, wq_hbm, wo_hbm, k_hbm, v_hbm, out_hbm,
-    wq, wo, kc, vc, xa, acc, js, jr, sqs, sqr, qs, at, ga, res,
+    wq, wo, kc, vc, xa, acc, js, jr, sqs, sqr, qs, at, ga, res, bias, fin,
     wq_sem, wo_sem, k_sem, v_sem,
     x_sz, x_sy, x_rv, j_sn, j_rv, q_sn, q_rv, a_sz, a_sy, a_rv, o_sn, o_rv,
 ):
@@ -89,11 +89,26 @@
             device_id={"wide": target}, device_id_type=MESH,
         )
 
-    def x_z(dz, c):
+    def x_z(dz, c, way):
+        b = (z - way * dz) * Y + y
         return remote(
-            xa.at[me, c], xa.at[me, c], x_sz.at[dz, c], x_rv.at[me, c],
-            lax.rem(z + dz, Z) * Y + y,
-        )
+            xa.at[b, c], xa.at[b, c], x_sz.at[dz * 2 + (way + 1) // 2, c], x_rv.at[b, c],
+            (z + way) * Y + y,
+        )
+
+    def x_on(dz, way):
+        source, onward = z - way * dz, z + way
+        return (source >= 0) & (source < Z) & (onward >= 0) & (onward < Z)
+
+    def x_pass(dz, c, way):
+        @pl.when(x_on(dz, way))
+        def _():
+            x_z(dz, c, way).start()
+
+    def x_sent(dz, c, way):
+        @pl.when(x_on(dz, way))
+        def _():
+            x_z(dz, c, way).wait_send()
 
     def x_y(zb, c):
         b = zb * Y + y
@@ -103,9 +118,9 @@
         remote(xa.at[b, c], xa.at[b, c], x_sy.at[0, c], x_rv.at[b, c], other).wait_recv()
 
     for c in range(C):
+        x_pass(0, c, 1)
+        x_pass(0, c, -1)
         x_y(z, c).start()
-        for dz in range(1, Z):
-            x_z(dz, c).start()
 
     def q_copy(step):
         o = lax.rem(me + step, n)
@@ -127,32 +142,35 @@
         total += piece(me, c)
     acc[...] = total
 
-    def other_line(c):
-        for dz in range(Z):
-            x_wait(lax.rem(z + dz, Z) * Y + (1 - y), c)
-        part = acc[...]
-        for dz in range(Z):
-            part += piece(lax.rem(z + dz, Z) * Y + (1 - y), c)
-        acc[...] = part
-
-    def gather_step(c, carry):
-        for dz in range(1, Z):
-            zb = lax.rem(z + dz, Z)
-            x_wait(zb * Y + y, c)
-            x_y(zb, c).start()
-        part = acc[...]
-        for dz in range(1, Z):
-            part += piece(lax.rem(z + dz, Z) * Y + y, c)
-        acc[...] = part
-
-        @pl.when(c > 0)
-        def _():
-            other_line(c - 1)
+    def gather_step(i, carry):
+        d, c = i // C + 1, lax.rem(i, C)
+        for way in (1, -1):
+            source = z - way * d
+
+            @pl.when((source >= 0) & (source < Z))
+            def _():
+                x_wait(source * Y + y, c)
+                x_pass(d, c, way)
+                x_y(source, c).start()
+
+        for way in (1, -1):
+            source = z - way * d
+
+            @pl.when((source >= 0) & (source < Z))
+            def _():
+                acc[...] += piece(source * Y + y, c)
+
+        for way in (1, -1):
+            source = z - way * (d - 1)
+
+            @pl.when((source >= 0) & (source < Z) & ((d > 1) | (way == 1)))
+            def _():
+                x_wait(source * Y + (1 - y), c)
+                acc[...] += piece(source * Y + (1 - y), c)
 
         return carry
 
-    lax.fori_loop(0, C, gather_step, 0)
-    other_line(C - 1)
+    lax.fori_loop(0, Z * C, gather_step, 0)
 
     by_slot = jnp.dot(to_slot, acc[...].astype(jnp.bfloat16), preferred_element_type=jnp.float32)
     for o in range(n):
@@ -175,6 +193,10 @@
     angle = position.astype(jnp.float32) * jnp.exp(-math.log(rope_base) * half)
     cosine = jnp.cos(angle)
     sine = jnp.where(lane_of < HDIM // 2, -jnp.sin(angle), jnp.sin(angle))
+    place = lax.broadcasted_iota(jnp.int32, (heads, kc.shape[1]), 1)
+    for r in range(own):
+        bias[r * heads : (r + 1) * heads] = jnp.where(place < len_ref[0, r], 0.0, masked_score)
+    fin[...] = acts_ref[0].astype(jnp.float32)
     k_copy.wait()
     v_copy.wait()
     wo_copy.wait()
@@ -219,34 +241,81 @@
             a_wait(g, zb * Y + y)
             a_y(g, zb).start()
 
-    span = kc.shape[1]
+    def o_copy(c):
+        return pltpu.make_async_remote_copy(
+            src_ref=res.at[c],
+            dst_ref=out_hbm.at[0, :, pl.ds(c * OC, OC)],
+            send_sem=o_sn.at[c],
+            recv_sem=o_rv.at[c],
+            device_id={"section": lax.rem(sec + 1, sections)},
+            device_id_type=MESH,
+        )
+
     score_scale = 1.0 / math.sqrt(HDIM)
-    place = lax.broadcasted_iota(jnp.int32, (heads, span), 1)
+    depth = heads * HDIM
+    stacked = own * heads
+
+    def queries_of(g):
+        return qs[:, g * heads : (g + 1) * heads, :].reshape(stacked, HDIM)
+
+    def spread(slab):
+        return jnp.broadcast_to(qs[:, slab : slab + 1, :], (own, heads, HDIM)).reshape(
+            stacked, HDIM
+        )
+
+    def scores_of(g):
+        lanes = slice(g * HDIM, (g + 1) * HDIM)
+        return jnp.concatenate(
+            [
+                lax.dot_general(
+                    qs[r, g * heads : (g + 1) * heads, :].astype(jnp.bfloat16), kc[r, :, lanes],
+                    (((1,), (1,)), ((), ())), preferred_element_type=jnp.float32,
+                )
+                for r in range(own)
+            ],
+            axis=0,
+        )
+
+    def mixed_of(g):
+        for dz in range(Z):
+            a_wait(g, lax.rem(z + dz, Z) * Y + (1 - y))
+        block = ga[g].astype(jnp.float32).reshape(rows, depth).astype(jnp.bfloat16)
+        return jnp.dot(to_request, block, preferred_element_type=jnp.float32).astype(jnp.bfloat16)
+
+    def project(g):
+        mixed = mixed_of(g)
+        for c in range(out_chunks):
+            at_cols = slice(c * OC, (c + 1) * OC)
+            fin[:, at_cols] += jnp.dot(
+                mixed, wo[g * depth : (g + 1) * depth, at_cols], preferred_element_type=jnp.float32
+            )
+
+    upcoming = scores_of(0)
     for g in range(G):
+        scores = upcoming
+        if g < G - 1:
+            upcoming = scores_of(g + 1)
         lanes = slice(g * HDIM, (g + 1) * HDIM)
-        for r in range(own):
-            query = qs[r, g * heads : (g + 1) * heads, :]
-            new_key = qs[r, HEADS + g : HEADS + g + 1, :]
-            new_value = qs[r, HEADS + G + g : HEADS + G + g + 1, :]
-            own_score = jnp.sum(query * new_key, axis=1, keepdims=True) * score_scale
-            scores = (
-                lax.dot_general(
-                    query.astype(jnp.bfloat16), kc[r, :, lanes], (((1,), (1,)), ((), ())),
+        own_score = (
+            jnp.sum(queries_of(g) * spread(HEADS + g), axis=1, keepdims=True) * score_scale
+        )
+        masked = scores * score_scale + bias[...]
+        peak = jnp.maximum(jnp.max(masked, axis=1, keepdims=True), own_score)
+        weights = jnp.exp(masked - peak)
+        own_weight = jnp.exp(own_score - peak)
+        denominator = jnp.sum(weights, axis=1, keepdims=True) + own_weight
+        weighted = jnp.concatenate(
+            [
+                jnp.dot(
+                    weights[r * heads : (r + 1) * heads].astype(jnp.bfloat16), vc[r, :, lanes],
                     preferred_element_type=jnp.float32,
                 )
-                * score_scale
-            )
-            live = place < len_ref[0, r]
-            masked = jnp.where(live, scores, masked_score)
-            peak = jnp.maximum(jnp.max(masked, axis=1, keepdims=True), own_score)
-            weights = jnp.where(live, jnp.exp(masked - peak), 0.0)
-            own_weight = jnp.exp(own_score - peak)
-            denominator = jnp.sum(weights, axis=1, keepdims=True) + own_weight
-            weighted = jnp.dot(
-                weights.astype(jnp.bfloat16), vc[r, :, lanes], preferred_element_type=jnp.float32
-            )
-            weighted += own_weight.astype(jnp.bfloat16).astype(jnp.float32) * new_value
-            at[g, r] = weighted / denominator
+                for r in range(own)
+            ],
+            axis=0,
+        )
+        weighted += own_weight.astype(jnp.bfloat16).astype(jnp.float32) * spread(HEADS + G + g)
+        at[g] = (weighted / denominator).reshape(own, heads, HDIM)
         for h in range(heads):
             ga[g, me, :, h * HDIM : (h + 1) * HDIM] = at[g, :, h, :].astype(jnp.bfloat16)
         a_y(g, z).start()
@@ -256,38 +325,23 @@
             relay(g - 2)
     for g in range(max(G - 2, 0), G):
         relay(g)
-
-    def o_copy(c):
-        return pltpu.make_async_remote_copy(
-            src_ref=res.at[c],
-            dst_ref=out_hbm.at[0, :, pl.ds(c * OC, OC)],
-            send_sem=o_sn.at[c],
-            recv_sem=o_rv.at[c],
-            device_id={"section": lax.rem(sec + 1, sections)},
-            device_id_type=MESH,
-        )
-
-    depth = heads * HDIM
-    mixed = []
-    for g in range(G):
-        for dz in range(Z):
-            a_wait(g, lax.rem(z + dz, Z) * Y + (1 - y))
-        block = ga[g].astype(jnp.float32).reshape(rows, depth).astype(jnp.bfloat16)
-        mixed.append(
-            jnp.dot(to_request, block, preferred_element_type=jnp.float32).astype(jnp.bfloat16)
-        )
-        if g == G - 1:
-            whole = jnp.concatenate(mixed, axis=1)
-            for c in range(out_chunks):
-                at_cols = slice(c * OC, (c + 1) * OC)
-                part = acts_ref[0, :, at_cols].astype(jnp.float32)
-                part += jnp.dot(whole, wo[:, at_cols], preferred_element_type=jnp.float32)
-                res[c] = part.astype(jnp.bfloat16)
-                o_copy(c).start()
+        if g < G - 1:
+            project(g - (G - 2))
+    for g in range(1, G - 1):
+        project(g)
+    mixed = mixed_of(G - 1)
+    for c in range(out_chunks):
+        at_cols = slice(c * OC, (c + 1) * OC)
+        part = fin[:, at_cols] + jnp.dot(
+            mixed, wo[(G - 1) * depth :, at_cols], preferred_element_type=jnp.float32
+        )
+        res[c] = part.astype(jnp.bfloat16)
+        o_copy(c).start()
 
     for c in range(C):
-        for dz in range(1, Z):
-            x_z(dz, c).wait_send()
+        for dz in range(Z - 1):
+            x_sent(dz, c, 1)
+            x_sent(dz, c, -1)
         for zb in range(Z):
             x_y(zb, c).wait_send()
     for step in range(1, n):
@@ -303,7 +357,7 @@
 
 
 def fused(n, sections, acts, norm_gain, w_qkv, w_out, key_cache, value_cache, cache_lengths, slot_of):
-    Y, C, out_chunks = 2, 4, 4
+    Y, C, out_chunks = 2, 2, 4
     rows, width = acts.shape[1:]
     own, span, kv_width = key_cache.shape[1:]
     cols = w_qkv.shape[2]
@@ -335,8 +389,10 @@
             pltpu.VMEM((G, own, heads, HDIM), f32),
             pltpu.VMEM((G, n, own, heads * HDIM), bf16),
             pltpu.VMEM((out_chunks, rows, width // out_chunks), bf16),
+            pltpu.VMEM((own * heads, span), f32),
+            pltpu.VMEM((rows, width), f32),
             dma((n,)), dma, dma, dma,
-            dma((Z, C)), dma((Z, C)), dma((n, C)),
+            dma((2 * Z, C)), dma((Z, C)), dma((n, C)),
             dma((n,)), dma((n,)), dma((n,)), dma((n,)),
             dma((G, Z)), dma((G, Z)), dma((G, n)),
             dma((out_chunks,)), dma((out_chunks,)),

time: 52.5 us -> 44.6 us (0.85)
  Pallas kernels: 50.8 us -> 42.8 us
    pallas_call x1, Pallas kernels: 50.8 us -> 42.8 us  [fused(): pl.pallas_call(functools.partial(tick, n, Y, C, sections), out_shape=jax....]
where the time goes in v2:
time: 44.6 us; the launch traced here: 44.4 us
  Pallas kernels  42.8 us (96%)
  local copies, waits for them, and re-layouts  1.57 us (4%)
    pallas_call x1, Pallas kernels, fused(): pl.pallas_call(functools.partial(tick, n, Y, C, sections), out_shape=jax....  42.8 us
    unnamed x1, local copies, waits for them, and re-layouts  1.57 us

profile of v2, /device:TPU:0, one launch (start us, length us, event | category | flops | bytes accessed | tf_op | source)
XLA Modules:
  0.0 44.4 jit_solution(10426577793287124195)
XLA Ops:
  0.0 42.8 %shard_map.82 = bf16[1,64,1024]{2,1,0:T(8,128)(2,1)} custom-call(bf16[1,64,1024]{2,1,0:T(8,128)(2,1)} %acts_ref.1, bf16[1,1024]{1,0:T(2,128)(2,1)} %gain_ref.1, s32[1,64]{1,0:T(1,128)} %slot_ref.1, s32[1,8]{1,0:T(1,128)} %len_ref.1, bf16[1,8192,640]{2,1,0:T(8,128)(2,1)} %wq_hbm.1, bf16[1,4096,1024]{2,1,0:T(8,128)(2,1)} %wo_hbm.1, ...), custom_call_target="tpu_custom_call" | custom-call | tf_op jit(solution)/shard_map/pallas_call | solution.py:372
  42.8 1.6 %copy.10 = bf16[1,64,1024]{2,1,0:T(8,128)(2,1)} copy(bf16[1,64,1024]{2,1,0:T(8,128)(2,1)} %shard_map.82) | data formatting | bytes 262144
